TPU v7x, 32 devices: a whole 2x2x4 slice. The times are simulated.
32 devices in a mesh: member: 8 (over y, x, core), tensor: 4 (over z).
Axes of the slice: x: 2, y: 2, z: 4, core: 2. Of those that a mesh axis runs over, the one named last changes fastest.
Arguments:
- prompt_acts: bfloat16 [128, 5120], P(None, 'member'), may hold values from -6 to 6
- gate_weight: bfloat16 [5120, 13824], P('member', 'tensor'), may hold values from -0.078125 to 0.078125
- up_weight: bfloat16 [5120, 13824], P('member', 'tensor'), may hold values from -0.078125 to 0.078125
- down_weight: bfloat16 [13824, 5120], P('tensor', 'member'), may hold values from -0.0546875 to 0.0546875
- d_table: bfloat16 [128, 3, 4, 5120], P('member'), may hold values from -6 to 6
- f_table: bfloat16 [128, 3, 4, 13824], P('member', None, None, 'tensor'), may hold values from -6 to 6
- seeds: int32 [64], P('member'), may hold values from 0 to 15
- fitness: float32 [64], P('member'), may hold values from -6 to 6
Outputs:
- outputs: bfloat16 [64, 128, 5120], P('member', None, 'tensor')
- delta_gate: bfloat16 [5120, 13824], P('member', 'tensor')
- delta_up: bfloat16 [5120, 13824], P('member', 'tensor')
- delta_down: bfloat16 [13824, 5120], P('tensor', 'member')
Inputs may be any that keep to these rules, and one draw needn't show every extreme that they name: Member m uses row (m // 8) * 16 + seeds[m] of both tables, a row in its own group's block.
All inputs are finite; a program needn't handle non-finite values.
Results may differ from a plain program's by a relative error of at most 0.025.
Values may be sent and summed in bfloat16 or wider, within the bound.
No kernel may reach another device: no remote copies, remote signals or barrier semaphores. Data moves between devices by JAX's collectives and lax.ppermute only.
A program may use at most 192 MiB of HBM per device.

v0:
```python
import math

import jax
import jax.numpy as jnp
from jax import lax
from jax.sharding import PartitionSpec as P

D = 5120
FFW = 13824


perturb_gain = 0.5


def shards(prompt_acts, gate_weight, up_weight, down_weight, d_table, f_table, seeds, fitness):
    members = seeds.shape[0]
    prompt_len = prompt_acts.shape[0]
    rank_size = d_table.shape[2]
    d_sel = jnp.take(d_table, seeds, axis=0)
    selected_factors = jnp.take(f_table, seeds, axis=0)
    d_slices = lax.all_to_all(d_sel, "member", split_axis=3, concat_axis=0, tiled=True)
    f_all, fit_all = (
        lax.all_gather(selected_factors, "member", axis=0, tiled=True),
        lax.all_gather(fitness.astype(jnp.bfloat16), "member", axis=0, tiled=True).astype(
            fitness.dtype
        ),
    )
    population = fit_all.shape[0]
    gate_part = jnp.dot(prompt_acts, gate_weight, preferred_element_type=jnp.float32)
    up_part = jnp.dot(prompt_acts, up_weight, preferred_element_type=jnp.float32)
    prompt_full = lax.all_gather(prompt_acts, "member", axis=1, tiled=True)
    gate_sum, up_sum = (
        lax.psum(gate_part.astype(jnp.bfloat16), "member").astype(jnp.float32),
        lax.psum(up_part.astype(jnp.bfloat16), "member").astype(jnp.float32),
    )
    in_factors = d_sel[:, :2].reshape(members * 2 * rank_size, D)
    proj_sum = jnp.dot(prompt_full, in_factors.T, preferred_element_type=jnp.float32)
    base_gate = gate_sum.astype(jnp.bfloat16)
    base_up = up_sum.astype(jnp.bfloat16)
    proj_inputs = (
        (proj_sum / math.sqrt(D)).astype(jnp.bfloat16).reshape(prompt_len, members, 2, rank_size)
    )
    perturbed = jnp.einsum(
        "pmkr,mkrf->mkpf", proj_inputs, selected_factors[:, :2], preferred_element_type=jnp.float32
    )
    gate = base_gate.astype(jnp.float32)[None] + perturb_gain * perturbed[:, 0]
    up = base_up.astype(jnp.float32)[None] + perturb_gain * perturbed[:, 1]
    hidden_state = (jax.nn.silu(gate) * up).astype(jnp.bfloat16)
    projection_here = jnp.einsum(
        "cdv,czv->cdz", hidden_state, selected_factors[:, 2], preferred_element_type=jnp.float32
    )
    proj_down = (lax.psum(projection_here, "tensor") / math.sqrt(FFW)).astype(jnp.bfloat16)
    hidden_rows = hidden_state.reshape(members * prompt_len, hidden_state.shape[2])
    partial_value = jnp.dot(
        hidden_rows,
        lax.all_gather(down_weight, "member", axis=1, tiled=True),
        preferred_element_type=jnp.float32,
    )
    summed = lax.psum_scatter(
        partial_value.astype(jnp.bfloat16), "tensor", scatter_dimension=1, tiled=True
    ).astype(jnp.float32)
    local_column_range = summed.shape[1]
    col_start = lax.axis_index("tensor") * local_column_range
    out_factor = lax.dynamic_slice_in_dim(d_sel[:, 2], col_start, local_column_range, 2)
    down_noise_delta = perturb_gain * jnp.einsum(
        "mpr,mrd->mpd", proj_down, out_factor, preferred_element_type=jnp.float32
    )
    outputs = (summed.reshape(members, prompt_len, local_column_range) + down_noise_delta).astype(
        jnp.bfloat16
    )
    mean = jnp.sum(fit_all) / population
    spread = jnp.sum((fit_all - mean) ** 2) / population
    score = (fit_all - mean) / jnp.sqrt(spread + 1.0)
    weighted = (d_slices.astype(jnp.float32) * score[:, None, None, None]).astype(jnp.bfloat16)
    scale = 1.0 / math.sqrt(population * rank_size)
    width_cols = weighted.shape[3]
    hidden_cols = f_all.shape[3]
    w_gate = weighted[:, 0].reshape(population * rank_size, width_cols)
    w_up = weighted[:, 1].reshape(population * rank_size, width_cols)
    w_down = weighted[:, 2].reshape(population * rank_size, width_cols)
    f_gate = f_all[:, 0].reshape(population * rank_size, hidden_cols)
    f_up = f_all[:, 1].reshape(population * rank_size, hidden_cols)
    down_factor_columns = f_all[:, 2].reshape(population * rank_size, hidden_cols)
    delta_gate = (jnp.dot(w_gate.T, f_gate, preferred_element_type=jnp.float32) * scale).astype(
        jnp.bfloat16
    )
    delta_up = (jnp.dot(w_up.T, f_up, preferred_element_type=jnp.float32) * scale).astype(
        jnp.bfloat16
    )
    delta_down = (
        jnp.dot(down_factor_columns.T, w_down, preferred_element_type=jnp.float32) * scale
    ).astype(jnp.bfloat16)
    return (outputs, delta_gate, delta_up, delta_down)


def solution(mesh):
    in_specs = (
        P(None, "member"),
        P("member", "tensor"),
        P("member", "tensor"),
        P("tensor", "member"),
        P("member", None, None, None),
        P("member", None, None, "tensor"),
        P("member"),
        P("member"),
    )
    out_specs = (
        P("member", None, "tensor"),
        P("member", "tensor"),
        P("member", "tensor"),
        P("tensor", "member"),
    )
    return jax.shard_map(shards, mesh=mesh, in_specs=in_specs, out_specs=out_specs, check_vma=False)
```

profile of v0, /device:TPU:0, one launch (start us, length us, event | category | flops | bytes accessed | tf_op | source)
XLA Modules:
  0.0 510.3 jit_solution(4729490581838769242)
XLA Ops:
  7.2 4.3 convolution_convert_fusion.1
  11.5 4.2 convolution_convert_fusion.2
  17.2 2.4 gather_fusion.1
  19.7 1.2 broadcast_select_fusion.1
  21.0 2.3 gather_fusion
  23.3 1.8 broadcast_select_fusion
  25.3 1.0 reshape.64
  26.3 52.1 %all-reduce.4.cloned.1.call-done = (bf16[128,3456]{1,0:T(8,128)(2,1)}, bf16[128,3456]{1,0:T(8,128)(2,1)}) async-done(((bf16[128,3456]{1,0:T(8,128)(2,1)}, bf16[128,3456]{1,0:T(8,128)(2,1)}), (bf16[128,3456]{1,0:T(8,128)(2,1)}, bf16[128,3456]{1,0:T(8,128)(2,1)})) %all-reduce.4.cloned.1.call-update) | async-done | bytes 1769488 | tf_op jit(solution)/shard_map/psum | solution.py:34
  78.5 1.3 convert_element_type.69
  79.8 3.1 convert_element_type.73
  82.9 21.3 %all-gather.4.cloned.1.call-done = bf16[128,5120]{1,0:T(8,128)(2,1)} async-done(((bf16[128,640]{1,0:T(8,128)(2,1)}), bf16[128,5120]{1,0:T(8,128)(2,1)}) %all-gather.4.cloned.1.call-update) | async-done | bytes 1310736 | tf_op jit(solution)/shard_map/all_gather | solution.py:31
  104.2 2.1 fusion.12
  106.2 18.7 %fusion.13 = f32[8,2,128,3456]{3,2,1,0:T(8,128)} fusion(bf16[128,8,2,4]{0,3,2,1:T(4,128)(2,1)S(1)} %bitcast.104, bf16[8,3,4,3456]{3,2,1,0:T(4,128)(2,1)} %broadcast_select_fusion.1), kind=kOutput, calls=%fused_computation.34 | convolution fusion | flops 56623104 | bytes 28770304 | tf_op jit(solution)/shard_map/pmkr,mkrf->mkpf/dot_general | solution.py:43
  125.0 11.1 %fusion = f32[8,1,128,3456]{3,2,0,1:T(8,128)} fusion(f32[8,2,128,3456]{3,2,1,0:T(8,128)} %fusion.13), kind=kLoop, calls=%fused_computation.4 | loop fusion | flops 3538944 | bytes 28311552 | tf_op jit(solution)/shard_map/mul | solution.py:46
  136.1 11.2 %slice_multiply_fusion = f32[8,1,128,3456]{3,2,1,0:T(8,128)} fusion(f32[8,2,128,3456]{3,2,1,0:T(8,128)} %fusion.13), kind=kLoop, calls=%fused_computation.2 | loop fusion | flops 3538944 | bytes 28311552 | tf_op jit(solution)/shard_map/mul | solution.py:47
  147.3 13.3 %fusion.4 = bf16[1024,3456]{1,0:T(8,128)(2,1)} fusion(f32[8,1,128,3456]{3,2,1,0:T(8,128)} %slice_multiply_fusion, f32[8,1,128,3456]{3,2,0,1:T(8,128)} %fusion, f32[128,3456]{1,0:T(8,128)} %convert_element_type.73, f32[128,3456]{1,0:T(8,128)S(1)} %convert_element_type.69), kind=kLoop, calls=%fused_computation.11 | loop fusion | flops 28311552 | bytes 38928384 | tf_op jit(solution)/shard_map/convert_element_type | solution.py:48
  160.6 114.7 %all-gather.6.cloned.1.call-done = bf16[3456,5120]{1,0:T(8,128)(2,1)} async-done(((bf16[3456,640]{1,0:T(8,128)(2,1)}), bf16[3456,5120]{1,0:T(8,128)(2,1)}) %all-gather.6.cloned.1.call-update) | async-done | bytes 35389456 | tf_op jit(solution)/shard_map/all_gather | solution.py:56
  275.2 45.1 %convolution_convert_fusion = bf16[1024,5120]{1,0:T(8,128)(2,1)} fusion(bf16[1024,3456]{1,0:T(8,128)(2,1)} %fusion.4, bf16[3456,5120]{1,0:T(8,128)(2,1)} %all-gather.6.cloned.1.call-done), kind=kOutput, calls=%fused_computation.13 | convolution fusion | flops 36244029440 | bytes 52953088 | tf_op jit(solution)/shard_map/dot_general | solution.py:54
  320.4 14.9 %copy.34 = bf16[8,3,4,5120]{0,2,1,3:T(4,128)(2,1)} copy(bf16[8,3,4,5120]{3,2,1,0:T(4,128)(2,1)S(1)} %broadcast_select_fusion) | data formatting | bytes 1966080 | tf_op jit(solution)/shard_map/jit(_take)/select_n | solution.py:19
  335.3 19.3 %reshape.104 = bf16[8,2,30720]{2,1,0:T(2,128)(2,1)} reshape(bf16[5120,3,4,8]{3,2,1,0:T(4,128)(2,1)} %bitcast.102) | data formatting | bytes 1966080
  354.6 3.6 all-to-all-start
  359.8 19.9 %all-reduce = bf16[64]{0:T(256)(128)(2,1)S(1)} all-reduce(bf16[64]{0:T(256)(128)(2,1)S(1)} %dynamic-update-slice), channel_id=1, replica_groups=mesh['member'=8,'tensor'=4] {'member'}, use_global_device_ids=true, to_apply=%add | all-reduce | flops 64 | bytes 256
  382.3 19.7 %reshape.105 = bf16[5120,3,4,8]{3,2,1,0:T(4,128)(2,1)} reshape(bf16[8,2,30720]{2,1,0:T(2,128)(2,1)S(1)} %all-to-all-done) | data formatting | bytes 1966080
  402.1 19.0 %copy.35 = f32[8,3,4,8,640]{4,0,3,2,1:T(8,128)S(1)} copy(bf16[8,3,4,8,640]{0,2,1,4,3:T(4,128)(2,1)} %bitcast.101) | data formatting | bytes 2949120 | tf_op jit(solution)/shard_map/convert_element_type | solution.py:74
  421.4 13.1 %fusion.8 = f32[8,128,4]{1,2,0:T(4,128)S(1)} fusion(f32[128,3456]{1,0:T(8,128)} %convert_element_type.73, f32[128,3456]{1,0:T(8,128)} %copy-done.3, bf16[8,3,4,3456]{3,2,1,0:T(4,128)(2,1)} %broadcast_select_fusion.1, f32[8,2,128,3456]{3,2,1,0:T(8,128)} %fusion.13), kind=kOutput, calls=%fused_computation.20 | convolution fusion | flops 63700992 | bytes 32088064 | tf_op jit(solution)/shard_map/cdv,czv->cdz/dot_general | solution.py:49
  434.4 20.0 %psum.23 = f32[8,128,4]{1,2,0:T(4,128)S(1)} all-reduce(f32[8,128,4]{1,2,0:T(4,128)S(1)} %fusion.8), channel_id=1, replica_groups=mesh['member'=8,'tensor'=4] {'tensor'}, use_global_device_ids=true, to_apply=%region_3.4 | all-reduce | flops 4096 | bytes 32768 | tf_op jit(solution)/shard_map/psum | solution.py:52
  454.4 3.6 fusion.23
  458.1 3.5 fusion.6
  461.5 3.5 fusion.7
  465.0 3.7 fusion.5
  468.7 30.9 %reduce-scatter.2.cloned.1.call-done = bf16[1024,1280]{1,0:T(8,128)(2,1)} async-done(((bf16[1024,5120]{1,0:T(8,128)(2,1)}), bf16[1024,1280]{1,0:T(8,128)(2,1)}) %reduce-scatter.2.cloned.1.call-update) | async-done | bytes 2621456 | tf_op jit(solution)/shard_map/reduce_scatter | solution.py:59
  499.6 4.2 fusion.10
  (40 shorter events, 4.4 us)
Async XLA Ops:
  7.2 13.8 %copy-start = (bf16[16,3,4,5120]{3,2,1,0:T(4,128)(2,1)S(1)}, bf16[16,3,4,5120]{3,2,1,0:T(4,128)(2,1)}, u32[]{:S(2)}) copy-start(bf16[16,3,4,5120]{3,2,1,0:T(4,128)(2,1)} %param.12) | copy-start | bytes 5898244
  7.2 71.3 %all-reduce.4.cloned.1.call-start = ((), (), s32[]{:S(2)}) async-start(), calls=%async_computation.6 | async-start | bytes 3538944 | tf_op jit(solution)/shard_map/psum | solution.py:34
  11.5 5.7 %copy-start.4 = (s32[8]{0:T(128)S(1)}, s32[8]{0:T(128)}, u32[]{:S(2)}) copy-start(s32[8]{0:T(128)} %param.14) | copy-start | bytes 100
  15.7 88.5 %all-gather.4.cloned.1.call-start = ((), (), s32[]{:S(2)}) async-start(), calls=%async_computation.2 | async-start | bytes 1474560 | tf_op jit(solution)/shard_map/all_gather | solution.py:31
  16.4 258.8 %all-gather.6.cloned.1.call-start = ((), (), s32[]{:S(2)}) async-start(), calls=%async_computation.3 | async-start | bytes 39813120 | tf_op jit(solution)/shard_map/all_gather | solution.py:56
  17.2 437.3 %all-gather.8.cloned.1.call-start = ((), (), s32[]{:S(2)}) async-start(), calls=%async_computation.5 | async-start | bytes 5971968 | tf_op jit(solution)/shard_map/all_gather | solution.py:23
  20.9 478.7 %reduce-scatter.2.cloned.1.call-start = ((), (), s32[]{:S(2)}) async-start(), calls=%async_computation.4 | async-start | bytes 13107200 | tf_op jit(solution)/shard_map/reduce_scatter | solution.py:59
  25.1 333.1 %copy-start.2 = (bf16[8,3,4,5120]{3,2,1,0:T(4,128)(2,1)}, bf16[8,3,4,5120]{3,2,1,0:T(4,128)(2,1)S(1)}, u32[]{:S(2)}) copy-start(bf16[8,3,4,5120]{3,2,1,0:T(4,128)(2,1)S(1)} %broadcast_select_fusion) | copy-start | bytes 2949124
  79.8 67.5 %copy-start.3 = (f32[128,3456]{1,0:T(8,128)}, f32[128,3456]{1,0:T(8,128)S(1)}, u32[]{:S(2)}) copy-start(f32[128,3456]{1,0:T(8,128)S(1)} %convert_element_type.69) | copy-start | bytes 5308420
  335.3 22.9 %copy-start.5 = (f32[8]{0:T(128)S(1)}, f32[8]{0:T(128)}, u32[]{:S(2)}) copy-start(f32[8]{0:T(128)} %param.15) | copy-start | bytes 100
  335.3 22.9 %copy-start.6 = (u32[32]{0:T(128)S(1)}, u32[32]{0:T(128)}, u32[]{:S(2)}) copy-start(u32[32]{0:T(128)} %constant.62) | copy-start | bytes 388
  354.6 27.7 %all-to-all-start = ((bf16[8,2,30720]{2,1,0:T(2,128)(2,1)}), bf16[8,2,30720]{2,1,0:T(2,128)(2,1)S(1)}, u32[]{:S(2)}, u32[]{:S(2)}) async-start(bf16[8,2,30720]{2,1,0:T(2,128)(2,1)} %reshape.104), calls=%async_computation.1 | async-start | bytes 1966080 | tf_op jit(solution)/shard_map/all_to_all | solution.py:21
  465.0 34.6 %slice-start = ((bf16[8,3,4,5120]{3,2,1,0:T(4,128)(2,1)}), bf16[8,1,4,5120]{3,2,1,0:T(4,128)(2,1)S(1)}, s32[]{:S(2)}) async-start(bf16[8,3,4,5120]{3,2,1,0:T(4,128)(2,1)} %copy-done.2), calls=%async_computation.7 | async-start | bytes 655360 | tf_op jit(solution)/shard_map/slice | solution.py:64
  465.0 38.8 %copy-start.1 = (bf16[16,3,4,5120]{3,2,1,0:T(4,128)(2,1)S(1)}, bf16[16,3,4,5120]{3,2,1,0:T(4,128)(2,1)}, u32[]{:S(2)}) copy-start(bf16[16,3,4,5120]{3,2,1,0:T(4,128)(2,1)} %param.12) | copy-start | bytes 5898244
Sparse Core Ops, SparseCore 0:
  15.8 62.6 all-reduce.3
  80.4 23.7 all-gather.3
  106.1 169.1 all-gather.5
  277.5 41.2 all-gather.7
  321.1 178.5 reduce-scatter.1
where the time goes:
time: 511 us; the launch traced here: 510 us
  waiting for transfers between devices  220 us (43%)
  matrix products  102 us (20%)
  local copies, waits for them, and re-layouts  83.5 us (16%)
  other arithmetic  44.6 us (9%)
  blocking collectives  39.9 us (8%)
  between operations  15.9 us (3%)
    all_gather x1, waiting for transfers between devices, shards(): lax.all_gather(down_weight, 'member', axis=1, tiled=True)  115 us
    psum x1, waiting for transfers between devices, shards(): lax.psum(up_part.astype(jnp.bfloat16), 'member').astype(jnp.float32)  52.1 us
    dot_general x1, matrix products, shards(): jnp.dot(hidden_rows, lax.all_gather(down_weight, 'member', axis=1, tiled=...  45.1 us
    unnamed x19, local copies, waits for them, and re-layouts  40 us
    reduce_scatter x1, waiting for transfers between devices, shards(): lax.psum_scatter(partial_value.astype(jnp.bfloat16), 'tensor', scatter_di...  30.9 us
    all_gather x1, waiting for transfers between devices, shards(): prompt_full = lax.all_gather(prompt_acts, 'member', axis=1, tiled=True)  21.3 us
    psum x1, blocking collectives, shards(): lax.psum(projection_here, 'tensor') / math.sqrt(FFW)  20 us
    unnamed x1, blocking collectives  19.9 us
  transfers between devices with their start and end apart: 6, of which 4 were waited for; matrix products, arithmetic and copies ran while one was open for 43% of the time, Pallas kernels for 0%

commit v1 on v0

v1 whole, which is shorter than its diff:
```python
import functools
import math

import jax
import jax.numpy as jnp
from jax import lax
from jax.experimental import pallas as pl
from jax.experimental.pallas import tpu as pltpu
from jax.sharding import PartitionSpec as P

perturb_gain = 0.5
CHUNKS = 4


def peer_of(own, shift, count):
    if count & (count - 1) == 0:
        return own ^ shift
    return (shift + count - own) % count


def home(pairs):
    return all(src == dst for src, dst in pairs)


def hidden_kernel(core_ref, base_ref, pg_ref, pu_ref, fac_ref, w_ref, out_ref, pd_ref, hid_ref, *, piece, copies):
    hidden_cols = w_ref.shape[0]
    rows4 = pg_ref.shape[2]
    prompt_len = base_ref.shape[1]

    def fill(step, carry):
        cols = pl.ds(pl.multiple_of(step * piece, piece), piece)
        fg = fac_ref[0, 0:rows4, cols]
        fu = fac_ref[0, rows4 : 2 * rows4, cols]
        bg = base_ref[0, :, cols].astype(jnp.float32)
        bu = base_ref[1, :, cols].astype(jnp.float32)
        for s in range(copies):
            rows = slice(s * prompt_len, (s + 1) * prompt_len)
            gate = bg + jnp.dot(pg_ref[0, rows, :], fg, preferred_element_type=jnp.float32)
            up = bu + jnp.dot(pu_ref[0, rows, :], fu, preferred_element_type=jnp.float32)
            half = 0.5 * gate
            hid_ref[rows, cols] = ((half + half * jnp.tanh(half)) * up).astype(jnp.bfloat16)
        return carry

    lax.fori_loop(0, hidden_cols // piece, fill, 0)
    out_ref[0] = jnp.dot(hid_ref[...], w_ref[...], preferred_element_type=jnp.float32).astype(jnp.bfloat16)
    pd_ref[0] = lax.dot_general(
        hid_ref[...],
        fac_ref[0, 2 * rows4 : 3 * rows4, :],
        (((1,), (1,)), ((), ())),
        preferred_element_type=jnp.float32,
    )


def partials(core, base, p_gate, p_up, factors, weights, chunk, chunk_rows, n_tensor, ratio):
    hidden_cols, out_cols = weights.shape
    prompt_len = base.shape[1]
    rows4 = p_gate.shape[2]
    piece = next((p for p in (384, 256, 128) if hidden_cols % p == 0), hidden_cols)
    group = lambda j, c: peer_of(c[1], j, n_tensor) * ratio + c[0]
    grid_spec = pltpu.PrefetchScalarGridSpec(
        num_scalar_prefetch=1,
        grid=(n_tensor,),
        in_specs=[
            pl.BlockSpec(base.shape, lambda j, c: (0, 0, 0)),
            pl.BlockSpec((1, chunk_rows, rows4), lambda j, c: (group(j, c), chunk, 0)),
            pl.BlockSpec((1, chunk_rows, rows4), lambda j, c: (group(j, c), chunk, 0)),
            pl.BlockSpec((1, 3 * rows4, hidden_cols), lambda j, c: (group(j, c), 0, 0)),
            pl.BlockSpec(weights.shape, lambda j, c: (0, 0)),
        ],
        out_specs=[
            pl.BlockSpec((1, chunk_rows, out_cols), lambda j, c: (j, 0, 0)),
            pl.BlockSpec((1, chunk_rows, rows4), lambda j, c: (j, 0, 0)),
        ],
        scratch_shapes=[pltpu.VMEM((chunk_rows, hidden_cols), jnp.bfloat16)],
    )
    flops = 2 * n_tensor * chunk_rows * hidden_cols * out_cols
    return pl.pallas_call(
        functools.partial(hidden_kernel, piece=piece, copies=chunk_rows // prompt_len),
        grid_spec=grid_spec,
        out_shape=[
            jax.ShapeDtypeStruct((n_tensor, chunk_rows, out_cols), jnp.bfloat16),
            jax.ShapeDtypeStruct((n_tensor, chunk_rows, rows4), jnp.float32),
        ],
        compiler_params=pltpu.CompilerParams(vmem_limit_bytes=56 * 1024 * 1024),
        cost_estimate=pl.CostEstimate(
            flops=2 * flops, bytes_accessed=2 * hidden_cols * out_cols, transcendentals=n_tensor * chunk_rows * hidden_cols
        ),
    )(core, base, p_gate, p_up, factors, weights)


def shards(
    prompt_acts, gate_weight, up_weight, down_weight, d_table, f_table, seeds, fitness, n_member, n_tensor
):
    members = seeds.shape[0]
    prompt_len = prompt_acts.shape[0]
    rank_size = d_table.shape[2]
    width = d_table.shape[3]
    width_cols = prompt_acts.shape[1]
    hidden_cols = gate_weight.shape[1]
    ffw = hidden_cols * n_tensor
    rows4 = members * rank_size
    ratio = n_member // n_tensor
    population = members * n_member
    my_member = lax.axis_index("member")
    my_tensor = lax.axis_index("tensor")
    core = my_member % ratio

    f_sel = jnp.take(f_table, seeds, axis=0, mode="clip")
    f_rows = f_sel.transpose(1, 0, 2, 3).reshape(3 * rows4, hidden_cols)
    f_all = lax.all_gather(f_rows, "member", axis=0, tiled=False)

    d_sel = jnp.take(d_table, seeds, axis=0, mode="clip")
    d_rows = d_sel.transpose(1, 0, 2, 3).reshape(3 * rows4, width)
    fit_hi = fitness.astype(jnp.bfloat16)
    fit_lo = (fitness - fit_hi.astype(jnp.float32)).astype(jnp.bfloat16)
    fit_rows = jnp.pad(jnp.stack([fit_hi, fit_lo]), ((0, 14), (0, width_cols - members)))
    d_send = jnp.stack(
        [
            jnp.concatenate([d_rows[:, k * width_cols : (k + 1) * width_cols], fit_rows], axis=0)
            for k in range(n_member)
        ]
    )
    d_recv = lax.all_to_all(d_send, "member", split_axis=0, concat_axis=0, tiled=True)

    gate_part = jnp.dot(prompt_acts, gate_weight, preferred_element_type=jnp.float32).astype(jnp.bfloat16)
    up_part = jnp.dot(prompt_acts, up_weight, preferred_element_type=jnp.float32).astype(jnp.bfloat16)
    in_rows = d_recv[:, : 2 * rows4].reshape(n_member * 2 * rows4, width_cols)
    proj_part = lax.dot_general(
        prompt_acts, in_rows, (((1,), (1,)), ((), ())), preferred_element_type=jnp.float32
    ).astype(jnp.bfloat16)
    sums_part = jnp.concatenate([gate_part, up_part, proj_part], axis=1)
    sum_cols = sums_part.shape[1]
    row_share = prompt_len // n_member
    sums_recv = lax.all_to_all(
        sums_part.reshape(n_member, row_share, sum_cols), "member", split_axis=0, concat_axis=0, tiled=True
    )
    col_scale = jnp.where(jnp.arange(sum_cols) < 2 * hidden_cols, 1.0, 1.0 / math.sqrt(width))
    sums_mine = (jnp.sum(sums_recv.astype(jnp.float32), axis=0) * col_scale).astype(jnp.bfloat16)
    sums = lax.all_gather(sums_mine, "member", axis=0, tiled=True)
    base = jnp.stack([sums[:, :hidden_cols], sums[:, hidden_cols : 2 * hidden_cols]])
    proj = sums[:, 2 * hidden_cols :].reshape(prompt_len, n_member, 2, rows4).transpose(2, 1, 0, 3)
    own_rows = (jnp.arange(rows4) // rank_size)[None, :] == jnp.arange(members)[:, None]
    masked = jnp.where(own_rows[None, None, :, None, :], perturb_gain * proj[:, :, None], 0.0).astype(jnp.bfloat16)
    masked = masked.reshape(2, n_member, members * prompt_len, rows4)

    if ratio == 1:
        weights = down_weight
    elif ratio == 2:
        other = lax.ppermute(down_weight, "member", [(g, g ^ 1) for g in range(n_member)])
        first = core == 0
        weights = jnp.concatenate(
            [jnp.where(first, down_weight, other), jnp.where(first, other, down_weight)], axis=1
        )
    else:
        weights = lax.all_gather(
            down_weight,
            "member",
            axis=1,
            tiled=True,
            axis_index_groups=[list(range(i, i + ratio)) for i in range(0, n_member, ratio)],
        )
    chunk_rows = members // CHUNKS * prompt_len
    own = my_member // ratio
    core_arg = jnp.stack([core, own]).astype(jnp.int32)
    swaps = [
        [(g, peer_of(g // ratio, shift, n_tensor) * ratio + g % ratio) for g in range(n_member)]
        for shift in range(n_tensor)
    ]
    own_slot = peer_of(own, own, n_tensor)
    summed, proj_here = [], []
    for chunk in range(CHUNKS):
        part, pd = partials(
            core_arg, base, masked[0], masked[1], f_all, weights, chunk, chunk_rows, n_tensor, ratio
        )
        proj_here.append(lax.dynamic_index_in_dim(pd, own_slot, 0, keepdims=False))
        moved = jnp.stack([
                part[shift] if home(swaps[shift]) else lax.ppermute(part[shift], "member", swaps[shift])
                for shift in range(n_tensor)
            ])
        ordered = [
            lax.dynamic_index_in_dim(moved, peer_of(own, chip, n_tensor), 0, keepdims=False)
            for chip in range(n_tensor)
        ]
        flat = jnp.concatenate(ordered, axis=0)
        summed.append(lax.psum_scatter(flat, "tensor", scatter_dimension=0, tiled=True))
    pd_all = jnp.concatenate(proj_here, axis=0).reshape(members, prompt_len, members, rank_size)
    pick = jnp.arange(members)[:, None] == jnp.arange(members)[None, :]
    pd_own = jnp.sum(jnp.where(pick[:, None, :, None], pd_all, 0.0), axis=2)
    proj_down = (lax.psum(pd_own, "tensor") / math.sqrt(ffw)).astype(jnp.bfloat16)
    out_cols = summed[0].shape[1]
    out_factor = lax.dynamic_slice_in_dim(d_sel[:, 2], my_tensor * out_cols, out_cols, 2)
    noise = perturb_gain * jnp.einsum("mpr,mrd->mpd", proj_down, out_factor, preferred_element_type=jnp.float32)
    total = jnp.concatenate(summed, axis=0).reshape(members, prompt_len, out_cols).astype(jnp.float32)
    outputs = (total + noise).astype(jnp.bfloat16)

    fit_recv = d_recv[:, 3 * rows4 : 3 * rows4 + 2, :members].astype(jnp.float32)
    fit_all = (fit_recv[:, 0] + fit_recv[:, 1]).reshape(population)
    mean = jnp.sum(fit_all) / population
    spread = jnp.sum((fit_all - mean) ** 2) / population
    score = (fit_all - mean) / jnp.sqrt(spread + 1.0)
    scale = 1.0 / math.sqrt(population * rank_size)
    row_score = jnp.repeat(score, rank_size).reshape(n_member, rows4, 1)
    ranks = population * rank_size
    d_part = lambda k: (d_recv[:, k * rows4 : (k + 1) * rows4].astype(jnp.float32) * row_score).astype(
        jnp.bfloat16
    ).reshape(ranks, width_cols)
    f_part = lambda k: f_all[:, k * rows4 : (k + 1) * rows4].reshape(ranks, hidden_cols)
    outer = lambda a, b: (
        lax.dot_general(a, b, (((0,), (0,)), ((), ())), preferred_element_type=jnp.float32) * scale
    ).astype(jnp.bfloat16)
    return (
        outputs,
        outer(d_part(0), f_part(0)),
        outer(d_part(1), f_part(1)),
        outer(f_part(2), d_part(2)),
    )


def solution(mesh):
    in_specs = (
        P(None, "member"),
        P("member", "tensor"),
        P("member", "tensor"),
        P("tensor", "member"),
        P("member", None, None, None),
        P("member", None, None, "tensor"),
        P("member"),
        P("member"),
    )
    out_specs = (
        P("member", None, "tensor"),
        P("member", "tensor"),
        P("member", "tensor"),
        P("tensor", "member"),
    )
    body = functools.partial(shards, n_member=mesh.shape["member"], n_tensor=mesh.shape["tensor"])
    return jax.shard_map(body, mesh=mesh, in_specs=in_specs, out_specs=out_specs, check_vma=False)
```

time: 511 us -> 469 us (0.918)
  Pallas kernels: 0 us -> 112 us
  matrix products: 102 us -> 24.7 us
  local copies, waits for them, and re-layouts: 83.5 us -> 26.8 us
  blocking collectives: 39.9 us -> 19.6 us
  starting transfers between devices: 3.75 us -> 23.6 us
  waiting for transfers between devices: 220 us -> 201 us
    pallas_call x0 -> x4, Pallas kernels: none -> 112 us  [partials(): pl.pallas_call(functools.partial(hidden_kernel, piece=piece, copies=chunk...]
    all_gather x3 -> x2, waiting for transfers between devices: 136 us -> 41.1 us  [the longest x1 38.1 us: shards(): f_all = lax.all_gather(f_rows, 'member', axis=0, tiled=False)]
    dot_general x7 -> x4, matrix products: 89.7 us -> 16 us  [the longest x3 15.6 us: shards(): lax.dot_general(a, b, (((0,), (0,)), ((), ())), preferred_element_type=jn...]
    ppermute x0 -> x13, waiting for transfers between devices: none -> 53.7 us  [the longest x12 50.4 us: shards(): lax.ppermute(part[shift], 'member', swaps[shift])]
    psum x1 -> x0, waiting for transfers between devices: 52.1 us -> none  [shards(): lax.psum(up_part.astype(jnp.bfloat16), 'member').astype(jnp.float32)]
    reduce_scatter x1 -> x4, waiting for transfers between devices: 30.9 us -> 71.5 us  [shards(): lax.psum_scatter(flat, 'tensor', scatter_dimension=0, tiled=True)]
    unnamed x19 -> x11, local copies, waits for them, and re-layouts: 40 us -> 0.81 us
    all_to_all x1 -> x2, waiting for transfers between devices: 0.01 us -> 34.6 us  [the longest x1 24.4 us: shards(): lax.all_to_all(sums_part.reshape(n_member, row_share, sum_cols), 'member'...]
  transfers between devices with their start and end apart: 6 -> 21, of which waited for: 4 -> 11; matrix products, arithmetic and copies ran while one was open for 43% -> 15% of each run, Pallas kernels for 0% -> 18%
where the time goes in v1:
time: 469 us; the launch traced here: 468 us
  waiting for transfers between devices  201 us (43%)
  Pallas kernels  112 us (24%)
  other arithmetic  44.3 us (9%)
  local copies, waits for them, and re-layouts  26.8 us (6%)
  matrix products  24.7 us (5%)
  starting transfers between devices  23.6 us (5%)
  blocking collectives  19.6 us (4%)
  between operations  15.8 us (3%)
    pallas_call x4, Pallas kernels, partials(): pl.pallas_call(functools.partial(hidden_kernel, piece=piece, copies=chunk...  112 us
    reduce_scatter x4, waiting for transfers between devices, shards(): lax.psum_scatter(flat, 'tensor', scatter_dimension=0, tiled=True)  71.5 us
    ppermute x12, waiting for transfers between devices, shards(): lax.ppermute(part[shift], 'member', swaps[shift])  50.4 us
    all_gather x1, waiting for transfers between devices, shards(): f_all = lax.all_gather(f_rows, 'member', axis=0, tiled=False)  38.1 us
    all_to_all x1, waiting for transfers between devices, shards(): lax.all_to_all(sums_part.reshape(n_member, row_share, sum_cols), 'member'...  24.4 us
    psum x1, blocking collectives, shards(): lax.psum(pd_own, 'tensor') / math.sqrt(ffw)  19.6 us
    dot_general x3, matrix products, shards(): lax.dot_general(a, b, (((0,), (0,)), ((), ())), preferred_element_type=jn...  15.6 us
    ppermute x12, starting transfers between devices, shards(): lax.ppermute(part[shift], 'member', swaps[shift])  14.1 us
  transfers between devices with their start and end apart: 21, of which 11 were waited for; matrix products, arithmetic and copies ran while one was open for 15% of the time, Pallas kernels for 18%

profile of v1, /device:TPU:0, one launch (start us, length us, event | category | flops | bytes accessed | tf_op | source)
XLA Modules:
  0.0 468.0 jit_solution(8233735557357453864)
XLA Ops:
  16.3 5.2 %all-to-all-start = ((bf16[8,112,640]{2,1,0:T(8,128)(2,1)}), bf16[8,112,640]{2,1,0:T(8,128)(2,1)}, u32[]{:S(2)}, u32[]{:S(2)}) async-start(bf16[8,112,640]{2,1,0:T(8,128)(2,1)} %fusion.29), calls=%async_computation | async-start | bytes 2293760 | tf_op jit(solution)/shard_map/all_to_all | solution.py:123
  21.5 3.1 convolution_convert_fusion
  24.6 3.1 convolution_convert_fusion.1
  27.7 10.3 %all-to-all-done = bf16[8,112,640]{2,1,0:T(8,128)(2,1)} async-done(((bf16[8,112,640]{2,1,0:T(8,128)(2,1)}), bf16[8,112,640]{2,1,0:T(8,128)(2,1)}, u32[]{:S(2)}, u32[]{:S(2)}) %all-to-all-start) | async-done | bytes 1146912 | tf_op jit(solution)/shard_map/all_to_all | solution.py:123
  40.9 3.6 all-to-all-start.1
  44.5 24.4 %all-to-all-done.1 = bf16[8,16,7424]{2,1,0:T(8,128)(2,1)S(1)} async-done(((bf16[8,16,7424]{2,1,0:T(8,128)(2,1)}), bf16[8,16,7424]{2,1,0:T(8,128)(2,1)S(1)}, u32[]{:S(2)}, u32[]{:S(2)}) %all-to-all-start.1) | async-done | bytes 1900576 | tf_op jit(solution)/shard_map/all_to_all | solution.py:134
  70.1 2.4 gather_fusion.1
  74.7 3.2 collective-permute-done
  77.9 7.9 %broadcast_select_fusion.1 = (bf16[3456,640]{1,0:T(8,128)(2,1)}, bf16[3456,640]{1,0:T(8,128)(2,1)}) fusion(bf16[3456,640]{1,0:T(8,128)(2,1)} %param.11, bf16[3456,640]{1,0:T(8,128)(2,1)} %collective-permute-done, pred[]{:T(512)S(6)} %eq.42), kind=kLoop, calls=%fused_computation.14 | loop fusion | flops 4423680 | bytes 17694720 | tf_op jit(solution)/shard_map/jit(_where)/select_n | solution.py:152
  85.8 8.0 %pad_maximum_fusion.w_ref = bf16[3456,1280]{1,0:T(8,128)(2,1)} fusion(bf16[3456,640]{1,0:T(8,128)(2,1)} %get-tuple-element.23, bf16[3456,640]{1,0:T(8,128)(2,1)} %get-tuple-element.22), kind=kLoop, calls=%fused_computation.2 | loop fusion | flops 17694720 | bytes 17694720 | tf_op jit(solution)/shard_map/concatenate | solution.py:151
  93.8 3.1 all-gather.3.cloned.1.call-done
  98.5 2.5 fusion.43
  102.6 38.1 %all-gather.5.cloned.1.call-done.fac_ref = bf16[8,96,3456]{2,1,0:T(8,128)(2,1)} async-done(((bf16[1,96,3456]{2,1,0:T(8,128)(2,1)}), bf16[8,96,3456]{2,1,0:T(8,128)(2,1)}) %all-gather.5.cloned.1.call-update) | async-done | bytes 5308432 | tf_op jit(solution)/shard_map/all_gather | solution.py:110
  140.7 27.9 %shard_map.111 = (bf16[4,256,1280]{2,1,0:T(8,128)(2,1)}, f32[4,256,32]{2,1,0:T(8,128)}) custom-call(s32[2]{0:T(128)} %pad_add_fusion.core_ref, bf16[2,128,3456]{2,1,0:T(8,128)(2,1)} %pad_maximum_fusion.11.base_ref, bf16[8,1024,32]{2,1,0:T(8,128)(2,1)} %bitcast.171, bf16[8,1024,32]{2,1,0:T(8,128)(2,1)} %bitcast.167, ...), custom_call_target="tpu_custom_call" | custom-call | flops 18119393280 | bytes 8847360 | tf_op jit(solution)/shard_map/pallas_call | solution.py:77
  168.6 2.7 fusion.44
  174.8 27.9 %shard_map.112 = (bf16[4,256,1280]{2,1,0:T(8,128)(2,1)}, f32[4,256,32]{2,1,0:T(8,128)}) custom-call(s32[2]{0:T(128)} %pad_add_fusion.core_ref, bf16[2,128,3456]{2,1,0:T(8,128)(2,1)} %pad_maximum_fusion.11.base_ref, bf16[8,1024,32]{2,1,0:T(8,128)(2,1)} %bitcast.172, bf16[8,1024,32]{2,1,0:T(8,128)(2,1)} %bitcast.168, ...), custom_call_target="tpu_custom_call" | custom-call | flops 18119393280 | bytes 8847360 | tf_op jit(solution)/shard_map/pallas_call | solution.py:77
  202.7 3.0 fusion.45
  211.0 12.6 %collective-permute-done.4 = bf16[256,1280]{1,0:T(8,128)(2,1)} collective-permute-done((bf16[256,1280]{1,0:T(8,128)(2,1)}, bf16[256,1280]{1,0:T(8,128)(2,1)}, u32[]{:S(2)}, u32[]{:S(2)}) %collective-permute-start.4) | collective-permute-done | bytes 655392 | tf_op jit(solution)/shard_map/ppermute | solution.py:177
  223.6 13.7 %collective-permute-done.5 = bf16[256,1280]{1,0:T(8,128)(2,1)} collective-permute-done((bf16[256,1280]{1,0:T(8,128)(2,1)}, bf16[256,1280]{1,0:T(8,128)(2,1)}, u32[]{:S(2)}, u32[]{:S(2)}) %collective-permute-start.5) | collective-permute-done | bytes 655392 | tf_op jit(solution)/shard_map/ppermute | solution.py:177
  242.0 2.6 pad_maximum_fusion.4
  244.9 28.4 %shard_map.113 = (bf16[4,256,1280]{2,1,0:T(8,128)(2,1)}, f32[4,256,32]{2,1,0:T(8,128)}) custom-call(s32[2]{0:T(128)} %pad_add_fusion.core_ref, bf16[2,128,3456]{2,1,0:T(8,128)(2,1)} %pad_maximum_fusion.11.base_ref, bf16[8,1024,32]{2,1,0:T(8,128)(2,1)} %bitcast.173, bf16[8,1024,32]{2,1,0:T(8,128)(2,1)} %bitcast.169, ...), custom_call_target="tpu_custom_call" | custom-call | flops 18119393280 | bytes 8847360 | tf_op jit(solution)/shard_map/pallas_call | solution.py:77
  278.8 27.9 %shard_map.114 = (bf16[4,256,1280]{2,1,0:T(8,128)(2,1)}, f32[4,256,32]{2,1,0:T(8,128)}) custom-call(s32[2]{0:T(128)} %pad_add_fusion.core_ref, bf16[2,128,3456]{2,1,0:T(8,128)(2,1)} %pad_maximum_fusion.11.base_ref, bf16[8,1024,32]{2,1,0:T(8,128)(2,1)} %bitcast.174, bf16[8,1024,32]{2,1,0:T(8,128)(2,1)} %bitcast.170, ...), custom_call_target="tpu_custom_call" | custom-call | flops 18119393280 | bytes 8847360 | tf_op jit(solution)/shard_map/pallas_call | solution.py:77
  312.5 13.8 %collective-permute-done.10 = bf16[256,1280]{1,0:T(8,128)(2,1)S(1)} collective-permute-done((bf16[256,1280]{1,0:T(8,128)(2,1)S(1)}, bf16[256,1280]{1,0:T(8,128)(2,1)S(1)}, u32[]{:S(2)}, u32[]{:S(2)}) %collective-permute-start.10) | collective-permute-done | bytes 655392 | tf_op jit(solution)/shard_map/ppermute | solution.py:177
  326.2 10.4 %collective-permute-done.11 = bf16[256,1280]{1,0:T(8,128)(2,1)S(1)} collective-permute-done((bf16[256,1280]{1,0:T(8,128)(2,1)S(1)}, bf16[256,1280]{1,0:T(8,128)(2,1)S(1)}, u32[]{:S(2)}, u32[]{:S(2)}) %collective-permute-start.11) | collective-permute-done | bytes 655392 | tf_op jit(solution)/shard_map/ppermute | solution.py:177
  339.8 2.6 pad_maximum_fusion.8
  350.2 19.6 %psum.7 = f32[8,128,4]{1,2,0:T(4,128)S(1)} all-reduce(f32[8,128,4]{1,2,0:T(4,128)S(1)} %copy.50), channel_id=1, replica_groups=mesh['member'=8,'tensor'=4] {'tensor'}, use_global_device_ids=true, to_apply=%region_6.7 | all-reduce | flops 4096 | bytes 32768 | tf_op jit(solution)/shard_map/psum | solution.py:189
  369.8 5.3 %fusion = bf16[3456,640]{1,0:T(8,128)(2,1)} fusion(bf16[8,96,3456]{2,1,0:T(8,128)(2,1)} %all-gather.5.cloned.1.call-done.fac_ref, bf16[8,112,640]{2,1,0:T(8,128)(2,1)} %all-to-all-done, f32[8,32]{1,0:T(8,128)S(1)} %copy.52), kind=kOutput, calls=%fused_computation.4 | convolution fusion | flops 1137377280 | bytes 6521856 | tf_op jit(solution)/shard_map/dot_general | solution.py:209
  375.1 5.2 %fusion.1 = bf16[640,3456]{1,0:T(8,128)(2,1)} fusion(bf16[8,96,3456]{2,1,0:T(8,128)(2,1)} %all-gather.5.cloned.1.call-done.fac_ref, bf16[8,112,640]{2,1,0:T(8,128)(2,1)} %all-to-all-done, f32[8,32]{1,0:T(8,128)S(1)} %copy.52), kind=kOutput, calls=%fused_computation.6 | convolution fusion | flops 1137377280 | bytes 6521856 | tf_op jit(solution)/shard_map/dot_general | solution.py:209
  380.2 5.2 %fusion.2 = bf16[640,3456]{1,0:T(8,128)(2,1)} fusion(bf16[8,96,3456]{2,1,0:T(8,128)(2,1)} %all-gather.5.cloned.1.call-done.fac_ref, bf16[8,112,640]{2,1,0:T(8,128)(2,1)} %all-to-all-done, f32[8,32]{1,0:T(8,128)S(1)} %copy.52), kind=kOutput, calls=%fused_computation.8 | convolution fusion | flops 1137377280 | bytes 6521856 | tf_op jit(solution)/shard_map/dot_general | solution.py:209
  385.4 16.9 %reduce-scatter.9.cloned.1.call-done = bf16[256,1280]{1,0:T(8,128)(2,1)} async-done(((bf16[1024,1280]{1,0:T(8,128)(2,1)}), bf16[256,1280]{1,0:T(8,128)(2,1)}) %reduce-scatter.9.cloned.1.call-update) | async-done | bytes 655376 | tf_op jit(solution)/shard_map/reduce_scatter | solution.py:185
  402.3 54.6 %reduce-scatter.11.cloned.1.call-done = bf16[256,1280]{1,0:T(8,128)(2,1)} async-done(((bf16[1024,1280]{1,0:T(8,128)(2,1)}), bf16[256,1280]{1,0:T(8,128)(2,1)}) %reduce-scatter.11.cloned.1.call-update) | async-done | bytes 655376 | tf_op jit(solution)/shard_map/reduce_scatter | solution.py:185
  458.7 2.4 fusion.3
  (109 shorter events, 54.5 us)
Async XLA Ops:
  7.2 1.6 copy-start
  10.1 0.7 copy-start.4
  10.8 10.6 %copy-start.3 = (bf16[128,640]{1,0:T(8,128)(2,1)S(1)}, bf16[128,640]{1,0:T(8,128)(2,1)}, u32[]{:S(2)}) copy-start(bf16[128,640]{1,0:T(8,128)(2,1)} %param.8) | copy-start | bytes 491524
  16.3 21.7 %all-to-all-start = ((bf16[8,112,640]{2,1,0:T(8,128)(2,1)}), bf16[8,112,640]{2,1,0:T(8,128)(2,1)}, u32[]{:S(2)}, u32[]{:S(2)}) async-start(bf16[8,112,640]{2,1,0:T(8,128)(2,1)} %fusion.29), calls=%async_computation | async-start | bytes 2293760 | tf_op jit(solution)/shard_map/all_to_all | solution.py:123
  40.9 28.0 %all-to-all-start.1 = ((bf16[8,16,7424]{2,1,0:T(8,128)(2,1)}), bf16[8,16,7424]{2,1,0:T(8,128)(2,1)S(1)}, u32[]{:S(2)}, u32[]{:S(2)}) async-start(bf16[8,16,7424]{2,1,0:T(8,128)(2,1)} %bitcast.163), calls=%async_computation.1 | async-start | bytes 3801088 | tf_op jit(solution)/shard_map/all_to_all | solution.py:134
  44.5 52.4 %all-gather.3.cloned.1.call-start = ((), (), s32[]{:S(2)}) async-start(), calls=%async_computation.6 | async-start | bytes 2138112 | tf_op jit(solution)/shard_map/all_gather | solution.py:139
  70.0 70.7 %all-gather.5.cloned.1.call-start = ((), (), s32[]{:S(2)}) async-start(), calls=%async_computation.7 | async-start | bytes 5971968 | tf_op jit(solution)/shard_map/all_gather | solution.py:110
  70.0 7.9 %collective-permute-start = (bf16[3456,640]{1,0:T(8,128)(2,1)}, bf16[3456,640]{1,0:T(8,128)(2,1)}, u32[]{:S(2)}, u32[]{:S(2)}) collective-permute-start(bf16[3456,640]{1,0:T(8,128)(2,1)} %param.11), channel_id=1, source_target_pairs={{0,4},{4,0},{8,12},{12,8},{16,20},{20,16},{24,28},{28,24},{1,5},{5... | collective-permute-start | bytes 13271048 | tf_op jit(solution)/shard_map/ppermute | solution.py:149
  73.8 311.6 %reduce-scatter.5.cloned.1.call-start = ((), (), s32[]{:S(2)}) async-start(), calls=%async_computation.8 | async-start | bytes 3276800 | tf_op jit(solution)/shard_map/reduce_scatter | solution.py:185
  98.5 2.5 copy-start.2
  171.3 36.4 %collective-permute-start.1 = (bf16[256,1280]{1,0:T(8,128)(2,1)S(1)}, bf16[256,1280]{1,0:T(8,128)(2,1)}, u32[]{:S(2)}, u32[]{:S(2)}) collective-permute-start(bf16[256,1280]{1,0:T(8,128)(2,1)S(1)} %get-tuple-element.33), channel_id=1, source_target_pairs={{0,8},{4,12},{8,0},{12,4},{16,24},{20,28},{24,16},{28,20},{1,9},{5... | collective-permute-start | bytes 1966088 | tf_op jit(solution)/shard_map/ppermute | solution.py:177
  172.8 36.4 %collective-permute-start.2 = (bf16[256,1280]{1,0:T(8,128)(2,1)}, bf16[256,1280]{1,0:T(8,128)(2,1)}, u32[]{:S(2)}, u32[]{:S(2)}) collective-permute-start(bf16[256,1280]{1,0:T(8,128)(2,1)} %get-tuple-element.32), channel_id=1, source_target_pairs={{0,16},{4,20},{8,24},{12,28},{16,0},{20,4},{24,8},{28,12},{1,17},{... | collective-permute-start | bytes 1966088 | tf_op jit(solution)/shard_map/ppermute | solution.py:177
  173.3 35.9 %collective-permute-start.3 = (bf16[256,1280]{1,0:T(8,128)(2,1)S(1)}, bf16[256,1280]{1,0:T(8,128)(2,1)}, u32[]{:S(2)}, u32[]{:S(2)}) collective-permute-start(bf16[256,1280]{1,0:T(8,128)(2,1)S(1)} %get-tuple-element.31), channel_id=1, source_target_pairs={{0,24},{4,28},{8,16},{12,20},{16,8},{20,12},{24,0},{28,4},{1,25},{... | collective-permute-start | bytes 1966088 | tf_op jit(solution)/shard_map/ppermute | solution.py:177
  205.7 17.9 %collective-permute-start.4 = (bf16[256,1280]{1,0:T(8,128)(2,1)}, bf16[256,1280]{1,0:T(8,128)(2,1)}, u32[]{:S(2)}, u32[]{:S(2)}) collective-permute-start(bf16[256,1280]{1,0:T(8,128)(2,1)} %get-tuple-element.41), channel_id=1, source_target_pairs={{0,8},{4,12},{8,0},{12,4},{16,24},{20,28},{24,16},{28,20},{1,9},{5... | collective-permute-start | bytes 1966088 | tf_op jit(solution)/shard_map/ppermute | solution.py:177
  207.2 30.1 %collective-permute-start.5 = (bf16[256,1280]{1,0:T(8,128)(2,1)}, bf16[256,1280]{1,0:T(8,128)(2,1)}, u32[]{:S(2)}, u32[]{:S(2)}) collective-permute-start(bf16[256,1280]{1,0:T(8,128)(2,1)} %get-tuple-element.40), channel_id=1, source_target_pairs={{0,16},{4,20},{8,24},{12,28},{16,0},{20,4},{24,8},{28,12},{1,17},{... | collective-permute-start | bytes 1966088 | tf_op jit(solution)/shard_map/ppermute | solution.py:177
  207.7 29.6 %collective-permute-start.6 = (bf16[256,1280]{1,0:T(8,128)(2,1)}, bf16[256,1280]{1,0:T(8,128)(2,1)}, u32[]{:S(2)}, u32[]{:S(2)}) collective-permute-start(bf16[256,1280]{1,0:T(8,128)(2,1)} %get-tuple-element.39), channel_id=1, source_target_pairs={{0,24},{4,28},{8,16},{12,20},{16,8},{20,12},{24,0},{28,4},{1,25},{... | collective-permute-start | bytes 1966088 | tf_op jit(solution)/shard_map/ppermute | solution.py:177
  241.9 143.5 %reduce-scatter.7.cloned.1.call-start = ((), (), s32[]{:S(2)}) async-start(), calls=%async_computation.9 | async-start | bytes 3276800 | tf_op jit(solution)/shard_map/reduce_scatter | solution.py:185
  244.7 157.6 %reduce-scatter.9.cloned.1.call-start = ((), (), s32[]{:S(2)}) async-start(), calls=%async_computation.10 | async-start | bytes 3276800 | tf_op jit(solution)/shard_map/reduce_scatter | solution.py:185
  275.2 35.1 %collective-permute-start.7 = (bf16[256,1280]{1,0:T(8,128)(2,1)S(1)}, bf16[256,1280]{1,0:T(8,128)(2,1)S(1)}, u32[]{:S(2)}, u32[]{:S(2)}) collective-permute-start(bf16[256,1280]{1,0:T(8,128)(2,1)S(1)} %get-tuple-element.49), channel_id=1, source_target_pairs={{0,8},{4,12},{8,0},{12,4},{16,24},{20,28},{24,16},{28,20},{1,9},{5... | collective-permute-start | bytes 1966088 | tf_op jit(solution)/shard_map/ppermute | solution.py:177
  275.8 36.3 %collective-permute-start.8 = (bf16[256,1280]{1,0:T(8,128)(2,1)S(1)}, bf16[256,1280]{1,0:T(8,128)(2,1)S(1)}, u32[]{:S(2)}, u32[]{:S(2)}) collective-permute-start(bf16[256,1280]{1,0:T(8,128)(2,1)S(1)} %get-tuple-element.48), channel_id=1, source_target_pairs={{0,16},{4,20},{8,24},{12,28},{16,0},{20,4},{24,8},{28,12},{1,17},{... | collective-permute-start | bytes 1966088 | tf_op jit(solution)/shard_map/ppermute | solution.py:177
  277.0 35.1 %collective-permute-start.9 = (bf16[256,1280]{1,0:T(8,128)(2,1)S(1)}, bf16[256,1280]{1,0:T(8,128)(2,1)S(1)}, u32[]{:S(2)}, u32[]{:S(2)}) collective-permute-start(bf16[256,1280]{1,0:T(8,128)(2,1)S(1)} %get-tuple-element.47), channel_id=1, source_target_pairs={{0,24},{4,28},{8,16},{12,20},{16,8},{20,12},{24,0},{28,4},{1,25},{... | collective-permute-start | bytes 1966088 | tf_op jit(solution)/shard_map/ppermute | solution.py:177
  308.6 17.7 %collective-permute-start.10 = (bf16[256,1280]{1,0:T(8,128)(2,1)S(1)}, bf16[256,1280]{1,0:T(8,128)(2,1)S(1)}, u32[]{:S(2)}, u32[]{:S(2)}) collective-permute-start(bf16[256,1280]{1,0:T(8,128)(2,1)S(1)} %get-tuple-element.57), channel_id=1, source_target_pairs={{0,8},{4,12},{8,0},{12,4},{16,24},{20,28},{24,16},{28,20},{1,9},{5... | collective-permute-start | bytes 1966088 | tf_op jit(solution)/shard_map/ppermute | solution.py:177
  309.1 27.5 %collective-permute-start.11 = (bf16[256,1280]{1,0:T(8,128)(2,1)S(1)}, bf16[256,1280]{1,0:T(8,128)(2,1)S(1)}, u32[]{:S(2)}, u32[]{:S(2)}) collective-permute-start(bf16[256,1280]{1,0:T(8,128)(2,1)S(1)} %get-tuple-element.56), channel_id=1, source_target_pairs={{0,16},{4,20},{8,24},{12,28},{16,0},{20,4},{24,8},{28,12},{1,17},{... | collective-permute-start | bytes 1966088 | tf_op jit(solution)/shard_map/ppermute | solution.py:177
  310.4 26.3 %collective-permute-start.12 = (bf16[256,1280]{1,0:T(8,128)(2,1)S(1)}, bf16[256,1280]{1,0:T(8,128)(2,1)S(1)}, u32[]{:S(2)}, u32[]{:S(2)}) collective-permute-start(bf16[256,1280]{1,0:T(8,128)(2,1)S(1)} %get-tuple-element.55), channel_id=1, source_target_pairs={{0,24},{4,28},{8,16},{12,20},{16,8},{20,12},{24,0},{28,4},{1,25},{... | collective-permute-start | bytes 1966088 | tf_op jit(solution)/shard_map/ppermute | solution.py:177
  339.8 117.1 %reduce-scatter.11.cloned.1.call-start = ((), (), s32[]{:S(2)}) async-start(), calls=%async_computation.11 | async-start | bytes 3276800 | tf_op jit(solution)/shard_map/reduce_scatter | solution.py:185
  458.7 2.4 copy-start.1
Sparse Core Ops, SparseCore 0:
  70.1 26.7 all-gather.2
  99.4 41.2 all-gather.4
  242.1 52.0 reduce-scatter.4
  296.3 51.7 reduce-scatter.6
  350.3 51.9 reduce-scatter.8
  405.0 51.8 reduce-scatter.10
